TPU v7x, 256 devices: a whole 4x4x8 slice. The times are simulated.
256 devices in a mesh: fsdp: 16 (over z, y_hi), cols: 16 (over y_lo, x, core).
Axes of the slice: x: 4, y: 4 (y_hi: 2, y_lo: 2; y = y_hi * 2 + y_lo), z: 8, core: 2. Of those that a mesh axis runs over, the one named last changes fastest.
Arguments:
- train_gate: bfloat16 [3584, 14336], P('fsdp', 'cols'), may hold values from -0.09375 to 0.09375
- low_gate: bfloat16 [3584, 16], P('fsdp'), may hold values from -0.09375 to 0.09375
- high_gate: bfloat16 [16, 14336], P(None, 'cols'), may hold values from -1.5 to 1.5
- train_up: bfloat16 [3584, 14336], P('fsdp', 'cols'), may hold values from -0.09375 to 0.09375
- low_up: bfloat16 [3584, 16], P('fsdp'), may hold values from -0.09375 to 0.09375
- high_up: bfloat16 [16, 14336], P(None, 'cols'), may hold values from -1.5 to 1.5
- train_down: bfloat16 [14336, 3584], P('cols', 'fsdp'), may hold values from -0.046875 to 0.046875
- low_down: bfloat16 [14336, 16], P('cols'), may hold values from -0.046875 to 0.046875
- high_down: bfloat16 [16, 3584], P(None, 'fsdp'), may hold values from -1.5 to 1.5
- norm_train: float32 [3584], P(('fsdp', 'cols')), may hold values from 0.25 to 1.75
- norm_step: float32 [3584], P(('fsdp', 'cols')), may hold values from -0.3 to 0.3
Outputs:
- serving_gate: bfloat16 [3584, 14336], P(None, 'cols')
- serving_up: bfloat16 [3584, 14336], P(None, 'cols')
- serving_down: bfloat16 [14336, 3584], P('cols')
- serve_norm: bfloat16 [3584], replicated
All inputs are finite; a program needn't handle non-finite values.
Results may differ from a plain program's by a relative error of at most 0.001.
Values may be sent and summed in bfloat16 or wider, within the bound.
A program may use at most 128 MiB of HBM per device.

v0:
```python
import functools

import jax
import jax.numpy as jnp
from jax import lax
from jax.experimental import pallas as pl
from jax.experimental.pallas import tpu as pltpu
from jax.sharding import PartitionSpec as P

MESH = pl.DeviceIdType.MESH
LANES = 128
SUBLANES = 16
mix_rate = 1.0


def merged(base, low, high):
    product = mix_rate * jnp.dot(low, high, preferred_element_type=jnp.float32)
    return (base.astype(jnp.float32) + product).astype(jnp.bfloat16)


def fold_of(width):
    fold = 1
    while width * fold % LANES:
        fold += 1
    return fold


def sends(k, depth, chunks):
    half = chunks // 2
    every, first, second = range(chunks), range(half), range(half, chunks)
    last = depth - 1
    down, up, side = [], [], [(k, 0, every)]
    if k > 0:
        down = [(z, 0, every) for z in range(k, depth)]
        if k == 1:
            down.append((k, 1, first))
        elif k == last:
            down.append((k, 1, every))
    if k < last:
        up = [(z, 0, every) for z in range(k, -1, -1)]
        if k == last - 1:
            up.append((k, 1, first))
        elif k == 0:
            up.append((k, 1, every))
    for z in sorted(set(range(depth)) - {k}, key=lambda z: abs(z - k)):
        if (k == 0 and z == 1) or (k == last and z == last - 1):
            side.append((z, 0, second))
        elif not (0 < k < last and ((k == 1 and z == 0) or (k == last - 1 and z == last))):
            side.append((z, 0, every))
    return [[(z, row, c) for z, row, cs in runs for c in cs] for runs in (down, up, side)]


def receives(k, depth, chunks):
    down = sends(k + 1, depth, chunks)[0] if k < depth - 1 else []
    up = sends(k - 1, depth, chunks)[1] if k > 0 else []
    side = [(z, 1 - row, c) for z, row, c in sends(k, depth, chunks)[2]]
    return [down, up, side]


def plan(k, depth, chunks):
    outs, ins = sends(k, depth, chunks), receives(k, depth, chunks)
    arrives = {item: (slot, s) for s, items in enumerate(ins) for slot, item in enumerate(items)}
    order = []
    for s, items in enumerate(outs):
        key = 0
        for slot, item in enumerate(items):
            if item[:2] != (k, 0):
                key = max(key, arrives[item][0] + 1, slot - 2)
            order.append((key, slot, s, item))
    return outs, ins, arrives, sorted(order)


def gather_kernel(n_fsdp, n_cols, parts, *refs):
    own = refs[:3]
    norm_ref = refs[3]
    out = refs[4:7]
    norms = refs[7]
    send_sem, recv_sem, local_sem, col_send, col_recv, row_send, row_recv = refs[8:]
    depth, chunks = n_fsdp // 2, 3 * parts
    here, col = lax.axis_index("fsdp"), lax.axis_index("cols")
    place, side = lax.div(here, 2), lax.rem(here, 2)

    barrier = pltpu.get_barrier_semaphore()
    for step in range(1, n_fsdp):
        peer = lax.rem(here + step, n_fsdp)
        pl.semaphore_signal(barrier, inc=1, device_id={"fsdp": peer}, device_id_type=MESH)
    for step in range(1, n_cols):
        peer = lax.rem(col + step, n_cols)
        pl.semaphore_signal(barrier, inc=1, device_id={"cols": peer}, device_id_type=MESH)
    pl.semaphore_wait(barrier, n_fsdp - 1 + n_cols - 1)

    def view(ref, c):
        rows = ref.shape[-2] // parts
        return pl.ds(c % parts * rows, rows)

    def landing(item):
        z, row, c = item
        block = 2 * z + (side if row == 0 else 1 - side)
        ref = out[c // parts]
        return ref.at[block, view(ref, c)]

    def source(k, item):
        z, row, c = item
        if (z, row) == (k, 0):
            ref = own[c // parts]
            return ref.at[view(ref, c)]
        return landing(item)

    def body(k):
        outs, ins, arrives, order = plan(k, depth, chunks)
        targets = (2 * (k - 1) + side, 2 * (k + 1) + side, 2 * k + 1 - side)
        waited = set()

        def copy(s, slot, item):
            return pltpu.make_async_remote_copy(
                src_ref=source(k, item),
                dst_ref=landing(item),
                send_sem=send_sem.at[s, slot],
                recv_sem=recv_sem.at[s, slot],
                device_id={"fsdp": targets[s]},
                device_id_type=MESH,
            )

        def arrive(s, slot):
            if (s, slot) in waited:
                return
            waited.add((s, slot))
            block = landing(ins[s][slot])
            pltpu.make_async_remote_copy(
                src_ref=block,
                dst_ref=block,
                send_sem=send_sem.at[s, slot],
                recv_sem=recv_sem.at[s, slot],
                device_id={"fsdp": targets[2]},
                device_id_type=MESH,
            ).wait_recv()

        for _, slot, s, item in order:
            if item[:2] != (k, 0):
                at, stream = arrives[item]
                arrive(stream, at)
            copy(s, slot, item).start()
        for slot in range(max(len(items) for items in ins)):
            for s in range(3):
                if slot < len(ins[s]):
                    arrive(s, slot)
        for s in range(3):
            for slot, item in enumerate(outs[s]):
                copy(s, slot, item).wait_send()

    mine = pltpu.make_async_copy(norm_ref, norms.at[here, col], local_sem.at[3])
    mine.start()
    for step in range(1, n_cols):
        pltpu.make_async_remote_copy(
            src_ref=norm_ref,
            dst_ref=norms.at[here, col],
            send_sem=col_send.at[step],
            recv_sem=col_recv.at[step],
            device_id={"cols": lax.rem(col + step, n_cols)},
            device_id_type=MESH,
        ).start()
    mine.wait()
    for step in range(1, n_cols):
        pltpu.make_async_remote_copy(
            src_ref=norm_ref,
            dst_ref=norms.at[here, lax.rem(col + n_cols - step, n_cols)],
            send_sem=col_send.at[step],
            recv_sem=col_recv.at[step],
            device_id={"cols": lax.rem(col + step, n_cols)},
            device_id_type=MESH,
        ).wait()

    def row_copy(step, block):
        return pltpu.make_async_remote_copy(
            src_ref=norms.at[here],
            dst_ref=norms.at[block],
            send_sem=row_send.at[step],
            recv_sem=row_recv.at[step],
            device_id={"fsdp": lax.rem(here + step, n_fsdp)},
            device_id_type=MESH,
        )

    for step in range(1, n_fsdp):
        row_copy(step, here).start()

    local = [pltpu.make_async_copy(own[a], out[a].at[here], local_sem.at[a]) for a in range(3)]
    for c in local:
        c.start()
    for k in range(depth):
        pl.when(place == k)(functools.partial(body, k))
    for c in local:
        c.wait()
    for step in range(1, n_fsdp):
        row_copy(step, lax.rem(here + n_fsdp - step, n_fsdp)).wait()


def gather(n_fsdp, n_cols, pieces, norm):
    parts = 2 if n_fsdp <= 8 else 1
    slots = 3 * parts * n_fsdp // 2
    anywhere = pl.BlockSpec(memory_space=pl.ANY)
    dma = pltpu.SemaphoreType.DMA
    return pl.pallas_call(
        functools.partial(gather_kernel, n_fsdp, n_cols, parts),
        out_shape=[jax.ShapeDtypeStruct((n_fsdp,) + p.shape, p.dtype) for p in pieces]
        + [jax.ShapeDtypeStruct((n_fsdp, n_cols) + norm.shape, norm.dtype)],
        in_specs=[anywhere] * 4,
        out_specs=[anywhere] * 4,
        scratch_shapes=[
            dma((3, slots)),
            dma((3, slots)),
            dma((4,)),
            dma((n_cols,)),
            dma((n_cols,)),
            dma((n_fsdp,)),
            dma((n_fsdp,)),
        ],
        compiler_params=pltpu.CompilerParams(collective_id=0, has_side_effects=True),
    )(*pieces, norm)


def unfold_kernel(fold, in_ref, out_ref):
    width = in_ref.shape[-1] // fold
    for p in range(fold):
        out_ref[p] = jnp.concatenate(
            [in_ref[0, j, :, p * width : (p + 1) * width] for j in range(fold)], axis=1
        )


def unfold(blocks, fold):
    count, rows, width = blocks.shape
    tile = next(t for t in (448, 224, 112, 16) if rows % t == 0)
    out = pl.pallas_call(
        functools.partial(unfold_kernel, fold),
        grid=(count // fold, rows // tile),
        out_shape=jax.ShapeDtypeStruct((fold, rows, count // fold * width), blocks.dtype),
        in_specs=[pl.BlockSpec((1, fold, tile, width), lambda z, r: (z, 0, r, 0))],
        out_specs=pl.BlockSpec((fold, tile, width), lambda z, r: (0, r, z)),
    )(blocks.reshape(count // fold, fold, rows, width))
    return out.reshape(fold * rows, -1)


def per_device(
    n_fsdp,
    n_cols,
    train_gate,
    low_gate,
    high_gate,
    train_up,
    low_up,
    high_up,
    train_down,
    low_down,
    high_down,
    norm_train,
    norm_step,
):
    gate = merged(train_gate, low_gate, high_gate)
    up = merged(train_up, low_up, high_up)
    down = merged(train_down, low_down, high_down)
    rows, width = down.shape
    fold = fold_of(width)
    down = jnp.concatenate(jnp.split(down, fold, axis=0), axis=1)
    length = norm_train.shape[0]
    norm = jnp.pad(norm_train + norm_step, (0, -length % LANES))
    norm = jnp.broadcast_to(norm[None], (8, norm.shape[0]))
    gates, ups, downs, norms = gather(n_fsdp, n_cols, (gate, up, down), norm)
    serve_norm = norms[:, :, 0, :length].reshape(-1).astype(jnp.bfloat16)
    return (
        gates.reshape(-1, gates.shape[-1]),
        ups.reshape(-1, ups.shape[-1]),
        unfold(downs, fold),
        serve_norm,
    )


def solution(mesh):
    return jax.shard_map(
        functools.partial(per_device, mesh.shape["fsdp"], mesh.shape["cols"]),
        mesh=mesh,
        in_specs=(
            P("fsdp", "cols"),
            P("fsdp", None),
            P(None, "cols"),
            P("fsdp", "cols"),
            P("fsdp", None),
            P(None, "cols"),
            P("cols", "fsdp"),
            P("cols", None),
            P(None, "fsdp"),
            P(("fsdp", "cols")),
            P(("fsdp", "cols")),
        ),
        out_specs=(P(None, "cols"), P(None, "cols"), P("cols", None), P()),
        check_vma=False,
    )
```

profile of v0, /device:TPU:1, one launch (start us, length us, event | category | flops | bytes accessed | tf_op | source)
XLA Modules:
  0.0 260.8 jit_solution(165605579274012535)
XLA Ops:
  0.6 0.0 copy-start
  0.6 0.7 add.17
  1.3 0.6 broadcast_in_dim.2.refs_3_
  1.9 0.0 copy-done
  1.9 2.1 fusion.1.refs_0_
  4.0 2.1 fusion.2.refs_1_
  6.1 1.2 copy.17
  7.3 1.1 fusion
  8.4 1.0 pad_maximum_fusion.refs_2_
  9.4 233.3 %shard_map.138 = (bf16[16,224,896]{2,1,0:T(8,128)(2,1)}, bf16[16,224,896]{2,1,0:T(8,128)(2,1)}, bf16[16,224,896]{2,1,0:T(8,128)(2,1)}, f32[16,16,8,128]{3,2,1,0:T(8,128)}) custom-call(bf16[224,896]{1,0:T(8,128)(2,1)} %fusion.1.refs_0_, bf16[224,896]{1,0:T(8,128)(2,1)} %fusion.2.refs_1_, bf16[224,896]{1,0:T(8,128)(2,1)} %pad_maximum_fusion.refs_2_, ...), custom_call_target="tpu_custom_call" | custom-call | tf_op jit(solution)/shard_map/pallas_call | solution.py:202
  242.6 1.6 fusion.3
  244.2 0.8 convert_element_type.30
  244.9 0.0 slice-start
  244.9 6.9 %shard_map.139 = bf16[4,224,3584]{2,1,0:T(8,128)(2,1)} custom-call(bf16[4,4,224,896]{3,2,1,0:T(8,128)(2,1)} %bitcast.15), custom_call_target="tpu_custom_call" | custom-call | tf_op jit(solution)/shard_map/pallas_call | solution.py:232
  251.8 0.0 slice-start.1
  251.8 6.2 %copy.22 = bf16[3584,896]{1,0:T(8,128)(2,1)} copy(bf16[3584,896]{1,0:T(8,128)(2,1)} %bitcast.14) | data formatting | bytes 12845056
  258.0 0.0 slice-done
  258.0 0.0 slice-done.1
  258.0 2.7 %copy.23 = bf16[3584,896]{1,0:T(8,128)(2,1)} copy(bf16[3584,896]{1,0:T(8,128)(2,1)S(1)} %bitcast.13) | data formatting | bytes 12845056
  (3 shorter events, 0.0 us)
Async XLA Ops:
  0.6 1.3 copy-start
  244.9 13.1 %slice-start = ((s8[6422528]{0:T(1024)(128)(4,1)}), s8[2228224]{0:T(1024)(128)(4,1)S(1)}, s32[]{:S(2)}) async-start(s8[6422528]{0:T(1024)(128)(4,1)} %bitcast.11), calls=%async_computation | async-start | bytes 4456448
  251.8 6.2 %slice-start.1 = ((s8[6422528]{0:T(1024)(128)(4,1)}), s8[4194304]{0:T(1024)(128)(4,1)S(1)}, s32[]{:S(2)}) async-start(s8[6422528]{0:T(1024)(128)(4,1)} %bitcast.11), calls=%async_computation.1 | async-start | bytes 8388608
where the time goes:
time: 265 us; the launch traced here: 261 us
  Pallas kernels  240 us (91%)
  local copies, waits for them, and re-layouts  13.1 us (5%)
  matrix products  5.22 us (2%)
    pallas_call x1, Pallas kernels, gather(): pl.pallas_call(functools.partial(gather_kernel, n_fsdp, n_cols, parts), o...  233 us
    unnamed x9, local copies, waits for them, and re-layouts  10.2 us
    pallas_call x1, Pallas kernels, unfold(): pl.pallas_call(functools.partial(unfold_kernel, fold), grid=(count // fol...  6.86 us

commit v1 on v0

v1 whole, which is shorter than its diff:
```python
import functools

import jax
import jax.numpy as jnp
from jax import lax
from jax.experimental import pallas as pl
from jax.experimental.pallas import tpu as pltpu
from jax.sharding import PartitionSpec as P

MESH = pl.DeviceIdType.MESH
LANES = 128
DEPTH = 8
PIECES = 3
mix_rate = 1.0

ORDER = (
    (0, 0, 0, 0), (1, 0, 0, 0), (2, 0, 0, 0), (0, 0, 0, 1), (1, 0, 0, 2), (2, 0, 0, 2),
    (0, 0, 7, 0), (1, 0, 1, 0), (2, 0, 1, 0), (0, 1, 0, 0), (1, 0, 1, 2), (2, 0, 1, 2),
    (0, 0, 6, 0), (1, 0, 2, 0), (2, 0, 2, 0), (1, 0, 0, 1), (0, 1, 7, 0), (2, 0, 2, 2),
    (0, 1, 0, 2), (2, 0, 5, 0), (0, 0, 5, 0), (2, 0, 0, 1), (0, 0, 7, 1), (1, 1, 2, 0),
    (2, 0, 1, 1), (2, 0, 7, 1), (1, 1, 2, 2), (1, 1, 3, 0), (0, 1, 7, 2), (1, 1, 3, 2),
    (1, 0, 2, 2), (0, 0, 6, 1), (2, 0, 6, 1), (1, 1, 1, 1), (1, 0, 1, 1), (0, 1, 6, 2),
    (2, 1, 4, 2), (2, 1, 7, 2), (0, 1, 6, 1), (0, 0, 5, 1), (1, 1, 2, 1), (2, 1, 5, 2),
    (2, 1, 6, 2), (0, 1, 5, 1), (1, 0, 2, 1),
)
SLOTS = len(ORDER) // 3


def received(port, column, offset, piece):
    if port == 0:
        return column, (offset - 1) % DEPTH, piece
    if port == 1:
        return column, (offset + 1) % DEPTH, piece
    return 1 - column, offset, piece


def plan():
    arrives, slots, sends = {}, [0, 0, 0], []
    for port, *item in ORDER:
        arrives[received(port, *item)] = (port, slots[port])
        sends.append((port, slots[port], tuple(item)))
        slots[port] += 1
    return sends, arrives


def gather_kernel(n_fsdp, n_cols, *refs):
    bases, lows, highs = refs[0:3], refs[3:6], refs[6:9]
    norm_train, norm_step = refs[9:11]
    gates, ups, downs, serve_norm = refs[11:15]
    turned, base_vm, low_vm, high_down, high_gate, high_up, train_vm, step_vm, parts, groups = refs[15:25]
    send_sem, recv_sem, local_sem, col_send, col_recv, row_send, row_recv = refs[25:]
    high_vm = (high_down, high_gate, high_up)
    wholes = (turned, gates, ups)
    rows = base_vm.shape[1]
    here, col = lax.axis_index("fsdp"), lax.axis_index("cols")
    place, side = lax.div(here, 2), lax.rem(here, 2)

    loads = [
        pltpu.make_async_copy(src, dst, local_sem.at[s])
        for s, (src, dst) in enumerate(
            [p for c in range(PIECES) for p in ((bases[c], base_vm.at[c]), (lows[c], low_vm.at[c]), (highs[c], high_vm[c]))]
            + [(norm_train, train_vm), (norm_step, step_vm)]
        )
    ]
    for load in loads:
        load.start()

    barrier = pltpu.get_barrier_semaphore()
    for step in range(1, n_fsdp):
        peer = lax.rem(here + step, n_fsdp)
        pl.semaphore_signal(barrier, inc=1, device_id={"fsdp": peer}, device_id_type=MESH)
    for step in range(1, n_cols):
        peer = lax.rem(col + step, n_cols)
        pl.semaphore_signal(barrier, inc=1, device_id={"cols": peer}, device_id_type=MESH)

    def block_of(column, offset):
        return 2 * lax.rem(place + offset, DEPTH) + (side if column == 0 else 1 - side)

    def where(column, offset, piece):
        start = pl.multiple_of(block_of(column, offset) * rows, 32)
        return wholes[piece].at[pl.ds(start, rows)]

    def merge(c):
        for load in loads[3 * c : 3 * c + 3]:
            load.wait()
        product = lax.dot_general(
            low_vm[c], high_vm[c][...], (((0,), (0,)), ((), ())), preferred_element_type=jnp.float32
        )
        where(0, 0, c)[...] = (base_vm[c].astype(jnp.float32) + mix_rate * product).astype(jnp.bfloat16)

    sends, arrives = plan()
    targets = (2 * lax.rem(place + 1, DEPTH) + side, 2 * lax.rem(place + DEPTH - 1, DEPTH) + side, 2 * place + 1 - side)

    def copy(port, slot, item):
        return pltpu.make_async_remote_copy(
            src_ref=where(*item),
            dst_ref=where(*item),
            send_sem=send_sem.at[port, slot],
            recv_sem=recv_sem.at[port, slot],
            device_id={"fsdp": targets[port]},
            device_id_type=MESH,
        )

    held = set()

    def hold(item):
        if item in held:
            return
        held.add(item)
        if item[:2] == (0, 0):
            merge(item[2])
        else:
            port, slot = arrives[item]
            copy(port, slot, item).wait_recv()

    def turn(w):
        window = turned[LANES * w : LANES * (w + 1), :]
        downs[:, LANES * w : LANES * (w + 1)] = window.T

    def norm_copy(block, peer_axis, step):
        if peer_axis == "cols":
            size, ref, me, s, r = n_cols, parts, col, col_send, col_recv
        else:
            size, ref, me, s, r = n_fsdp, groups, here, row_send, row_recv
        return pltpu.make_async_remote_copy(
            src_ref=ref.at[me],
            dst_ref=ref.at[block],
            send_sem=s.at[step],
            recv_sem=r.at[step],
            device_id={peer_axis: lax.rem(me + step, size)},
            device_id_type=MESH,
        )

    length = train_vm.shape[0]
    span = n_cols * length

    def norm_first():
        loads[-2].wait()
        loads[-1].wait()
        flat = LANES * lax.broadcasted_iota(jnp.int32, (8, LANES), 0) + lax.broadcasted_iota(jnp.int32, (8, LANES), 1)
        first = lax.rem(here * span, LANES) + col * length
        tile = jnp.zeros((8, LANES), jnp.float32)
        for j in range(length):
            tile = jnp.where(flat == first + j, train_vm[j] + step_vm[j], tile)
        parts[col] = tile
        for step in range(1, n_cols):
            norm_copy(col, "cols", step).start()

    def norm_second():
        for step in range(1, n_cols):
            norm_copy(lax.rem(col + n_cols - step, n_cols), "cols", step).wait()
        total = parts[0]
        for c in range(1, n_cols):
            total = total + parts[c]
        groups[here] = total
        for step in range(1, n_fsdp):
            norm_copy(here, "fsdp", step).start()

    def norm_third():
        for step in range(1, n_fsdp):
            norm_copy(lax.rem(here + n_fsdp - step, n_fsdp), "fsdp", step).wait()
        lines = serve_norm.shape[0]
        out = [None] * lines
        for g in range(n_fsdp):
            line = g * span // LANES
            for r in range(-(-(g * span % LANES + span) // LANES)):
                value = groups[g, r : r + 1, :]
                out[line + r] = value if out[line + r] is None else out[line + r] + value
        serve_norm[...] = jnp.concatenate(out, axis=0).astype(serve_norm.dtype)

    hold((0, 0, 0))
    pl.semaphore_wait(barrier, n_fsdp - 1 + n_cols - 1)
    downs_in = [item for item in arrives if item[2] == 0]
    windows = list(range(n_fsdp * rows // LANES))
    ready = None
    for at, (port, slot, item) in enumerate(sends):
        hold(item)
        copy(port, slot, item).start()
        if at == 5:
            norm_first()
        if at == 12:
            norm_second()
        if at == 18:
            norm_third()
        if ready is None and at > 25 and all(i in held for i in downs_in):
            ready = at
        if at == 30:
            for i in downs_in:
                hold(i)
            ready = at
        if ready is not None:
            for w in windows[:2]:
                turn(w)
            del windows[:2]
    for w in windows:
        turn(w)
    for item in arrives:
        hold(item)
    for port, slot, item in sends:
        copy(port, slot, item).wait_send()


def gather(n_fsdp, n_cols, bases, lows, highs, norm_train, norm_step):
    rows, width = bases[0].shape
    rank = lows[0].shape[0]
    anywhere = pl.BlockSpec(memory_space=pl.ANY)
    inside = pl.BlockSpec(memory_space=pltpu.VMEM)
    dma = pltpu.SemaphoreType.DMA
    bf16, f32 = jnp.bfloat16, jnp.float32
    lines = n_fsdp * n_cols * norm_train.shape[0] // LANES
    return pl.pallas_call(
        functools.partial(gather_kernel, n_fsdp, n_cols),
        out_shape=[
            pltpu.VMEM((n_fsdp * rows, width), bf16),
            pltpu.VMEM((n_fsdp * rows, width), bf16),
            pltpu.VMEM((width, n_fsdp * rows), bf16),
            pltpu.VMEM((lines, LANES), bf16),
        ],
        in_specs=[anywhere] * 11,
        out_specs=[inside] * 4,
        scratch_shapes=[
            pltpu.VMEM((n_fsdp * rows, width), bf16),
            pltpu.VMEM((PIECES, rows, width), bf16),
            pltpu.VMEM((PIECES, rank, rows), bf16),
            pltpu.VMEM((rank, width), bf16),
            pltpu.VMEM((rank, width), bf16),
            pltpu.VMEM((rank, width), bf16),
            pltpu.SMEM(norm_train.shape, f32),
            pltpu.SMEM(norm_step.shape, f32),
            pltpu.VMEM((n_cols, 8, LANES), f32),
            pltpu.VMEM((n_fsdp, 8, LANES), f32),
            dma((3, SLOTS)),
            dma((3, SLOTS)),
            dma((3 * PIECES + 2,)),
            dma((n_cols,)),
            dma((n_cols,)),
            dma((n_fsdp,)),
            dma((n_fsdp,)),
        ],
        compiler_params=pltpu.CompilerParams(collective_id=0, has_side_effects=True, vmem_limit_bytes=42 * 2**20),
    )(*bases, *lows, *highs, norm_train, norm_step)


def write_kernel(*refs):
    ins, outs, sem = refs[:3], refs[3:6], refs[6]
    parts = sem.shape[1]
    copies = []
    for a in range(3):
        rows = ins[a].shape[0] // parts
        for p in range(parts):
            part = pl.ds(p * rows, rows)
            copies.append(pltpu.make_async_copy(ins[a].at[part], outs[a].at[part], sem.at[a, p]))
    for c in copies:
        c.start()
    for c in copies:
        c.wait()


def write(arrays):
    return pl.pallas_call(
        write_kernel,
        out_shape=[jax.ShapeDtypeStruct(a.shape, a.dtype) for a in arrays],
        in_specs=[pl.BlockSpec(memory_space=pltpu.VMEM)] * 3,
        out_specs=[pl.BlockSpec(memory_space=pl.ANY)] * 3,
        scratch_shapes=[pltpu.SemaphoreType.DMA((3, 4))],
        compiler_params=pltpu.CompilerParams(vmem_limit_bytes=8 * 2**20),
    )(*arrays)


def per_device(
    n_fsdp,
    n_cols,
    train_gate,
    low_gate,
    high_gate,
    train_up,
    low_up,
    high_up,
    train_down,
    low_down,
    high_down,
    norm_train,
    norm_step,
):
    gates, ups, downs, norm = gather(
        n_fsdp,
        n_cols,
        (train_down.T, train_gate, train_up),
        (high_down, low_gate.T, low_up.T),
        (low_down.T, high_gate, high_up),
        norm_train,
        norm_step,
    )
    gates, ups, downs = write((gates, ups, downs))
    return gates, ups, downs, norm.reshape(-1)


def solution(mesh):
    return jax.shard_map(
        functools.partial(per_device, mesh.shape["fsdp"], mesh.shape["cols"]),
        mesh=mesh,
        in_specs=(
            P("fsdp", "cols"),
            P("fsdp", None),
            P(None, "cols"),
            P("fsdp", "cols"),
            P("fsdp", None),
            P(None, "cols"),
            P("cols", "fsdp"),
            P("cols", None),
            P(None, "fsdp"),
            P(("fsdp", "cols")),
            P(("fsdp", "cols")),
        ),
        out_specs=(P(None, "cols"), P(None, "cols"), P("cols", None), P()),
        check_vma=False,
    )
```

time: 265 us -> 151 us (0.57); the launches traced: 261 us -> 151 us
  Pallas kernels: 240 us -> 150 us
  local copies, waits for them, and re-layouts: 13.1 us -> 0.6 us
  matrix products: 5.22 us -> 0 us
    pallas_call x2, Pallas kernels: 240 us -> 150 us  [the longest x1 143 us: gather(): pl.pallas_call(functools.partial(gather_kernel, n_fsdp, n_cols), out_shap...]
    unnamed x9 -> x1, local copies, waits for them, and re-layouts: 10.2 us -> 0.6 us
    dot_general x3 -> x0, matrix products: 5.22 us -> none  [merged(): product = mix_rate * jnp.dot(low, high, preferred_element_type=jnp.float32)]
where the time goes in v1:
time: 151 us
  Pallas kernels  150 us (99%)
    pallas_call x1, Pallas kernels, gather(): pl.pallas_call(functools.partial(gather_kernel, n_fsdp, n_cols), out_shap...  143 us
    pallas_call x1, Pallas kernels, write(): pl.pallas_call(write_kernel, out_shape=[jax.ShapeDtypeStruct(a.shape, a.d...  6.71 us

profile of v1, /device:TPU:1, one launch (start us, length us, event | category | flops | bytes accessed | tf_op | source)
XLA Modules:
  0.0 151.2 jit_solution(7309953190443594360)
XLA Ops:
  0.6 143.3 %shard_map.138 = (bf16[3584,896]{1,0:T(8,128)(2,1)S(1)}, bf16[3584,896]{1,0:T(8,128)(2,1)S(1)}, bf16[896,3584]{1,0:T(8,128)(2,1)S(1)}, bf16[28,128]{1,0:T(8,128)(2,1)S(1)}) custom-call(bf16[224,896]{1,0:T(8,128)(2,1)} %bitcast.6, bf16[224,896]{1,0:T(8,128)(2,1)} %refs_1_.1, bf16[224,896]{1,0:T(8,128)(2,1)} %refs_2_.1, bf16[16,224]{1,0:T(8,128)(2,1)} %refs_3_.1, ...), custom_call_target="tpu_custom_call" | custom-call | tf_op jit(solution)/shard_map/pallas_call | solution.py:211
  143.9 6.7 %shard_map.139 = (bf16[3584,896]{1,0:T(8,128)(2,1)}, bf16[3584,896]{1,0:T(8,128)(2,1)}, bf16[896,3584]{1,0:T(8,128)(2,1)}) custom-call(bf16[3584,896]{1,0:T(8,128)(2,1)S(1)} %get-tuple-element.11.refs_0_, bf16[3584,896]{1,0:T(8,128)(2,1)S(1)} %get-tuple-element.12.refs_1_, bf16[896,3584]{1,0:T(8,128)(2,1)S(1)} %get-tuple-element.13.refs_2_), custom_call_target="tpu_custom_call" | custom-call | tf_op jit(solution)/shard_map/pallas_call | solution.py:260
  150.6 0.6 copy.16

commit v2 on v1

--- a/solution.py
+++ b/solution.py
@@ -24,6 +24,8 @@
     (2, 1, 6, 2), (0, 1, 5, 1), (1, 0, 2, 1),
 )
 SLOTS = len(ORDER) // 3
+NORM_AT = (6, 8, 10, 12)
+WRITES = 4
 
 
 def received(port, column, offset, piece):
@@ -43,12 +45,27 @@
     return sends, arrives
 
 
+def partners_of(col):
+    core, x, y = lax.rem(col, 2), lax.rem(lax.div(col, 2), 4), lax.div(col, 8)
+    odd = lax.rem(x, 2)
+
+    def at(y, x, core):
+        return (4 * y + x) * 2 + core
+
+    return (
+        at(y, x, 1 - core),
+        at(y, x + 1 - 2 * odd, core),
+        at(y, lax.rem(x + 3 + 2 * odd, 4), core),
+        at(1 - y, x, core),
+    )
+
+
 def gather_kernel(n_fsdp, n_cols, *refs):
     bases, lows, highs = refs[0:3], refs[3:6], refs[6:9]
     norm_train, norm_step = refs[9:11]
     gates, ups, downs, serve_norm = refs[11:15]
-    turned, base_vm, low_vm, high_down, high_gate, high_up, train_vm, step_vm, parts, groups = refs[15:25]
-    send_sem, recv_sem, local_sem, col_send, col_recv, row_send, row_recv = refs[25:]
+    turned, base_vm, low_vm, high_down, high_gate, high_up, train_vm, step_vm, sums, parts, groups = refs[15:26]
+    send_sem, recv_sem, local_sem, col_send, col_recv, row_send, row_recv = refs[26:]
     high_vm = (high_down, high_gate, high_up)
     wholes = (turned, gates, ups)
     rows = base_vm.shape[1]
@@ -66,11 +83,11 @@
         load.start()
 
     barrier = pltpu.get_barrier_semaphore()
-    for step in range(1, n_fsdp):
-        peer = lax.rem(here + step, n_fsdp)
+    targets = (2 * lax.rem(place + 1, DEPTH) + side, 2 * lax.rem(place + DEPTH - 1, DEPTH) + side, 2 * place + 1 - side)
+    for peer in targets:
         pl.semaphore_signal(barrier, inc=1, device_id={"fsdp": peer}, device_id_type=MESH)
-    for step in range(1, n_cols):
-        peer = lax.rem(col + step, n_cols)
+    partners = partners_of(col)
+    for peer in partners:
         pl.semaphore_signal(barrier, inc=1, device_id={"cols": peer}, device_id_type=MESH)
 
     def block_of(column, offset):
@@ -89,7 +106,6 @@
         where(0, 0, c)[...] = (base_vm[c].astype(jnp.float32) + mix_rate * product).astype(jnp.bfloat16)
 
     sends, arrives = plan()
-    targets = (2 * lax.rem(place + 1, DEPTH) + side, 2 * lax.rem(place + DEPTH - 1, DEPTH) + side, 2 * place + 1 - side)
 
     def copy(port, slot, item):
         return pltpu.make_async_remote_copy(
@@ -117,48 +133,54 @@
         window = turned[LANES * w : LANES * (w + 1), :]
         downs[:, LANES * w : LANES * (w + 1)] = window.T
 
-    def norm_copy(block, peer_axis, step):
-        if peer_axis == "cols":
-            size, ref, me, s, r = n_cols, parts, col, col_send, col_recv
-        else:
-            size, ref, me, s, r = n_fsdp, groups, here, row_send, row_recv
-        return pltpu.make_async_remote_copy(
-            src_ref=ref.at[me],
-            dst_ref=ref.at[block],
-            send_sem=s.at[step],
-            recv_sem=r.at[step],
-            device_id={peer_axis: lax.rem(me + step, size)},
-            device_id_type=MESH,
-        )
-
     length = train_vm.shape[0]
     span = n_cols * length
-
-    def norm_first():
-        loads[-2].wait()
-        loads[-1].wait()
-        flat = LANES * lax.broadcasted_iota(jnp.int32, (8, LANES), 0) + lax.broadcasted_iota(jnp.int32, (8, LANES), 1)
-        first = lax.rem(here * span, LANES) + col * length
-        tile = jnp.zeros((8, LANES), jnp.float32)
-        for j in range(length):
-            tile = jnp.where(flat == first + j, train_vm[j] + step_vm[j], tile)
-        parts[col] = tile
-        for step in range(1, n_cols):
-            norm_copy(col, "cols", step).start()
-
-    def norm_second():
-        for step in range(1, n_cols):
-            norm_copy(lax.rem(col + n_cols - step, n_cols), "cols", step).wait()
-        total = parts[0]
-        for c in range(1, n_cols):
-            total = total + parts[c]
-        groups[here] = total
+    tall = -(-(span + LANES - 1) // LANES)
+
+    def exchange(step):
+        return pltpu.make_async_remote_copy(
+            src_ref=sums.at[step, pl.ds(0, tall)],
+            dst_ref=parts.at[step, pl.ds(0, tall)],
+            send_sem=col_send.at[step],
+            recv_sem=col_recv.at[step],
+            device_id={"cols": partners[step]},
+            device_id_type=MESH,
+        )
+
+    def norm_step_at(step):
+        if step == 0:
+            loads[-2].wait()
+            loads[-1].wait()
+            flat = LANES * lax.broadcasted_iota(jnp.int32, (8, LANES), 0) + lax.broadcasted_iota(jnp.int32, (8, LANES), 1)
+            first = lax.rem(here * span, LANES) + col * length
+            tile = jnp.zeros((8, LANES), jnp.float32)
+            for j in range(length):
+                tile = jnp.where(flat == first + j, train_vm[j] + step_vm[j], tile)
+            sums[0] = tile
+        else:
+            exchange(step - 1).wait()
+            sums[step, 0:tall] = sums[step - 1, 0:tall] + parts[step - 1, 0:tall]
+        exchange(step).start()
+
+    def norm_copy(block, step):
+        return pltpu.make_async_remote_copy(
+            src_ref=groups.at[here, pl.ds(0, tall)],
+            dst_ref=groups.at[block, pl.ds(0, tall)],
+            send_sem=row_send.at[step],
+            recv_sem=row_recv.at[step],
+            device_id={"fsdp": lax.rem(here + step, n_fsdp)},
+            device_id_type=MESH,
+        )
+
+    def norm_spread():
+        exchange(3).wait()
+        groups[here, 0:tall] = sums[3, 0:tall] + parts[3, 0:tall]
         for step in range(1, n_fsdp):
-            norm_copy(here, "fsdp", step).start()
-
-    def norm_third():
+            norm_copy(here, step).start()
+
+    def norm_last():
         for step in range(1, n_fsdp):
-            norm_copy(lax.rem(here + n_fsdp - step, n_fsdp), "fsdp", step).wait()
+            norm_copy(lax.rem(here + n_fsdp - step, n_fsdp), step).wait()
         lines = serve_norm.shape[0]
         out = [None] * lines
         for g in range(n_fsdp):
@@ -169,25 +191,22 @@
         serve_norm[...] = jnp.concatenate(out, axis=0).astype(serve_norm.dtype)
 
     hold((0, 0, 0))
-    pl.semaphore_wait(barrier, n_fsdp - 1 + n_cols - 1)
+    pl.semaphore_wait(barrier, len(targets) + len(partners))
     downs_in = [item for item in arrives if item[2] == 0]
     windows = list(range(n_fsdp * rows // LANES))
     ready = None
     for at, (port, slot, item) in enumerate(sends):
         hold(item)
         copy(port, slot, item).start()
-        if at == 5:
-            norm_first()
-        if at == 12:
-            norm_second()
-        if at == 18:
-            norm_third()
-        if ready is None and at > 25 and all(i in held for i in downs_in):
-            ready = at
+        if at in NORM_AT:
+            norm_step_at(NORM_AT.index(at))
         if at == 30:
             for i in downs_in:
                 hold(i)
             ready = at
+            norm_spread()
+        if at == 43:
+            norm_last()
         if ready is not None:
             for w in windows[:2]:
                 turn(w)
@@ -227,13 +246,14 @@
             pltpu.VMEM((rank, width), bf16),
             pltpu.SMEM(norm_train.shape, f32),
             pltpu.SMEM(norm_step.shape, f32),
-            pltpu.VMEM((n_cols, 8, LANES), f32),
+            pltpu.VMEM((4, 8, LANES), f32),
+            pltpu.VMEM((4, 8, LANES), f32),
             pltpu.VMEM((n_fsdp, 8, LANES), f32),
             dma((3, SLOTS)),
             dma((3, SLOTS)),
             dma((3 * PIECES + 2,)),
-            dma((n_cols,)),
-            dma((n_cols,)),
+            dma((4,)),
+            dma((4,)),
             dma((n_fsdp,)),
             dma((n_fsdp,)),
         ],
@@ -242,12 +262,12 @@
 
 
 def write_kernel(*refs):
-    ins, outs, sem = refs[:3], refs[3:6], refs[6]
+    ins, outs, sem = refs[:4], refs[4:8], refs[8]
     parts = sem.shape[1]
-    copies = []
-    for a in range(3):
-        rows = ins[a].shape[0] // parts
-        for p in range(parts):
+    copies = [pltpu.make_async_copy(ins[3], outs[3], sem.at[3, 0])]
+    for p in range(parts):
+        for a in range(3):
+            rows = ins[a].shape[0] // parts
             part = pl.ds(p * rows, rows)
             copies.append(pltpu.make_async_copy(ins[a].at[part], outs[a].at[part], sem.at[a, p]))
     for c in copies:
@@ -260,9 +280,9 @@
     return pl.pallas_call(
         write_kernel,
         out_shape=[jax.ShapeDtypeStruct(a.shape, a.dtype) for a in arrays],
-        in_specs=[pl.BlockSpec(memory_space=pltpu.VMEM)] * 3,
-        out_specs=[pl.BlockSpec(memory_space=pl.ANY)] * 3,
-        scratch_shapes=[pltpu.SemaphoreType.DMA((3, 4))],
+        in_specs=[pl.BlockSpec(memory_space=pltpu.VMEM)] * 4,
+        out_specs=[pl.BlockSpec(memory_space=pl.ANY)] * 4,
+        scratch_shapes=[pltpu.SemaphoreType.DMA((4, WRITES))],
         compiler_params=pltpu.CompilerParams(vmem_limit_bytes=8 * 2**20),
     )(*arrays)
 
@@ -291,7 +311,7 @@
         norm_train,
         norm_step,
     )
-    gates, ups, downs = write((gates, ups, downs))
+    gates, ups, downs, norm = write((gates, ups, downs, norm))
     return gates, ups, downs, norm.reshape(-1)
 
 

time: 151 us -> 148 us (0.980)
  Pallas kernels: 150 us -> 147 us
    pallas_call x1, Pallas kernels: 143 us -> 140 us  [gather(): pl.pallas_call(functools.partial(gather_kernel, n_fsdp, n_cols), out_shap...]
where the time goes in v2:
time: 148 us
  Pallas kernels  147 us (99%)
    pallas_call x1, Pallas kernels, gather(): pl.pallas_call(functools.partial(gather_kernel, n_fsdp, n_cols), out_shap...  140 us
    pallas_call x1, Pallas kernels, write(): pl.pallas_call(write_kernel, out_shape=[jax.ShapeDtypeStruct(a.shape, a.d...  6.75 us

profile of v2, /device:TPU:1, one launch (start us, length us, event | category | flops | bytes accessed | tf_op | source)
XLA Modules:
  0.0 147.7 jit_solution(15934016479639885656)
XLA Ops:
  0.6 140.3 %shard_map.138 = (bf16[3584,896]{1,0:T(8,128)(2,1)S(1)}, bf16[3584,896]{1,0:T(8,128)(2,1)S(1)}, bf16[896,3584]{1,0:T(8,128)(2,1)S(1)}, bf16[28,128]{1,0:T(8,128)(2,1)S(1)}) custom-call(bf16[224,896]{1,0:T(8,128)(2,1)} %bitcast.5, bf16[224,896]{1,0:T(8,128)(2,1)} %refs_1_.1, bf16[224,896]{1,0:T(8,128)(2,1)} %refs_2_.1, bf16[16,224]{1,0:T(8,128)(2,1)} %refs_3_.1, ...), custom_call_target="tpu_custom_call" | custom-call | tf_op jit(solution)/shard_map/pallas_call | solution.py:230
  141.0 6.7 %shard_map.139 = (bf16[3584,896]{1,0:T(8,128)(2,1)}, bf16[3584,896]{1,0:T(8,128)(2,1)}, bf16[896,3584]{1,0:T(8,128)(2,1)}, bf16[28,128]{1,0:T(8,128)(2,1)}) custom-call(bf16[3584,896]{1,0:T(8,128)(2,1)S(1)} %get-tuple-element.12.refs_0_, bf16[3584,896]{1,0:T(8,128)(2,1)S(1)} %get-tuple-element.13.refs_1_, bf16[896,3584]{1,0:T(8,128)(2,1)S(1)} %get-tuple-element.14.refs_2_, ...), custom_call_target="tpu_custom_call" | custom-call | tf_op jit(solution)/shard_map/pallas_call | solution.py:280

commit v3 on v2

v3 whole, which is shorter than its diff:
```python
import functools

import jax
import jax.numpy as jnp
from jax import lax
from jax.experimental import pallas as pl
from jax.experimental.pallas import tpu as pltpu
from jax.sharding import PartitionSpec as P

MESH = pl.DeviceIdType.MESH
LANES = 128
DEPTH = 8
mix_rate = 1.0

WHOLE = (
    (0, 0, 0, 0), (1, 0, 0, 0), (2, 0, 0, 0), (0, 0, 0, 1), (1, 0, 0, 2), (2, 0, 0, 2),
    (0, 0, 7, 0), (1, 0, 1, 0), (2, 0, 1, 0), (0, 1, 0, 0), (1, 0, 1, 2), (2, 0, 1, 2),
    (0, 0, 6, 0), (1, 0, 2, 0), (2, 0, 2, 0), (1, 0, 0, 1), (0, 1, 7, 0), (2, 0, 2, 2),
    (0, 1, 0, 2), (2, 0, 5, 0), (0, 0, 5, 0), (2, 0, 0, 1), (0, 0, 7, 1), (1, 1, 2, 0),
    (2, 0, 1, 1), (2, 0, 7, 1), (1, 1, 2, 2), (1, 1, 3, 0), (0, 1, 7, 2), (1, 1, 3, 2),
    (1, 0, 2, 2), (0, 0, 6, 1), (2, 0, 6, 1), (1, 1, 1, 1), (1, 0, 1, 1), (0, 1, 6, 2),
    (2, 1, 4, 2), (2, 1, 7, 2), (0, 1, 6, 1), (0, 0, 5, 1), (1, 1, 2, 1), (2, 1, 5, 2),
    (2, 1, 6, 2), (0, 1, 5, 1), (1, 0, 2, 1),
)
FIRST = (
    (0, 0, 0, 0), (1, 0, 0, 0), (2, 0, 0, 0), (0, 0, 0, 1), (1, 0, 0, 1), (2, 0, 0, 1),
    (0, 0, 7, 0), (1, 0, 1, 0), (2, 0, 1, 0), (2, 0, 7, 0), (0, 0, 7, 1), (1, 0, 1, 1),
    (0, 0, 6, 0), (2, 0, 6, 0), (1, 1, 1, 0), (1, 0, 2, 0), (0, 0, 6, 1), (2, 0, 6, 1),
    (0, 0, 5, 0), (1, 1, 2, 0), (2, 0, 5, 0), (1, 0, 2, 1), (2, 0, 2, 1), (1, 1, 0, 1),
    (2, 0, 7, 1), (0, 1, 6, 1), (0, 1, 5, 0), (0, 1, 5, 1), (1, 0, 3, 1), (2, 0, 3, 1),
)
SECOND = (
    (0, 0, 0, 1), (1, 0, 0, 0), (2, 0, 0, 1), (0, 0, 0, 0), (1, 0, 0, 1), (2, 0, 0, 0),
    (0, 0, 7, 1), (1, 0, 1, 0), (2, 0, 7, 1), (1, 1, 0, 1), (0, 0, 7, 0), (2, 0, 7, 0),
    (1, 1, 0, 0), (0, 0, 6, 1), (2, 0, 6, 1), (1, 0, 2, 0), (2, 0, 2, 0), (0, 0, 6, 0),
    (1, 1, 1, 1), (2, 0, 6, 0), (1, 0, 1, 1), (0, 0, 5, 1), (2, 0, 3, 0), (2, 0, 5, 1),
    (0, 0, 5, 0), (1, 1, 2, 1), (0, 0, 4, 1), (2, 0, 4, 1), (0, 1, 6, 0), (1, 1, 3, 0),
)
NORM_AT = (8, 10, 12)


def received(port, column, offset, chunk):
    if port == 0:
        return column, (offset - 1) % DEPTH, chunk
    if port == 1:
        return column, (offset + 1) % DEPTH, chunk
    return 1 - column, offset, chunk


def plan(order):
    arrives, slots, sends = {}, [0, 0, 0], []
    for port, *item in order:
        arrives[received(port, *item)] = (port, slots[port])
        sends.append((port, slots[port], tuple(item)))
        slots[port] += 1
    return sends, arrives


def partners_of(col):
    core, x, y = lax.rem(col, 2), lax.rem(lax.div(col, 2), 4), lax.div(col, 8)
    odd = lax.rem(x, 2)

    def at(y, x, core):
        return (4 * y + x) * 2 + core

    return (
        at(y, x, 1 - core),
        at(y, x + 1 - 2 * odd, core),
        at(y, lax.rem(x + 3 + 2 * odd, 4), core),
        at(1 - y, x, core),
    )


def targets_of(here):
    place, side = lax.div(here, 2), lax.rem(here, 2)
    return (
        2 * lax.rem(place + 1, DEPTH) + side,
        2 * lax.rem(place + DEPTH - 1, DEPTH) + side,
        2 * place + 1 - side,
    )


class Exchange:
    def __init__(self, order, bases, lows, highs, base_vm, low_vm, high_vm, wholes, send_sem, recv_sem, load_sem):
        self.sends, self.arrives = plan(order)
        self.wholes, self.base_vm, self.low_vm, self.high_vm = wholes, base_vm, low_vm, high_vm
        self.send_sem, self.recv_sem = send_sem, recv_sem
        self.rows = base_vm.shape[1]
        self.parts = (max(item[2] for item in self.arrives) + 1) // len(wholes)
        here = lax.axis_index("fsdp")
        self.place, self.side = lax.div(here, 2), lax.rem(here, 2)
        self.targets = targets_of(here)
        self.held = set()
        self.merged = set()
        self.loads = []
        for c in range(len(wholes)):
            for n, (src, dst) in enumerate(((bases[c], base_vm.at[c]), (lows[c], low_vm.at[c]), (highs[c], high_vm.at[c]))):
                self.loads.append(pltpu.make_async_copy(src, dst, load_sem.at[c, n]))
        for load in self.loads:
            load.start()

    def where(self, column, offset, chunk):
        size = self.rows // self.parts
        block = 2 * lax.rem(self.place + offset, DEPTH) + (self.side if column == 0 else 1 - self.side)
        start = pl.multiple_of(block * self.rows + chunk % self.parts * size, 16)
        return self.wholes[chunk // self.parts].at[pl.ds(start, size)]

    def merge(self, c):
        if c in self.merged:
            return
        self.merged.add(c)
        for load in self.loads[3 * c : 3 * c + 3]:
            load.wait()
        product = lax.dot_general(
            self.low_vm[c], self.high_vm[c], (((0,), (0,)), ((), ())), preferred_element_type=jnp.float32
        )
        value = (self.base_vm[c].astype(jnp.float32) + mix_rate * product).astype(jnp.bfloat16)
        start = pl.multiple_of((2 * self.place + self.side) * self.rows, 16)
        self.wholes[c][pl.ds(start, self.rows), :] = value

    def copy(self, port, slot, item):
        return pltpu.make_async_remote_copy(
            src_ref=self.where(*item),
            dst_ref=self.where(*item),
            send_sem=self.send_sem.at[port, slot],
            recv_sem=self.recv_sem.at[port, slot],
            device_id={"fsdp": self.targets[port]},
            device_id_type=MESH,
        )

    def hold(self, item):
        if item in self.held:
            return
        self.held.add(item)
        if item[:2] == (0, 0):
            self.merge(item[2] // self.parts)
        else:
            port, slot = self.arrives[item]
            self.copy(port, slot, item).wait_recv()

    def send(self, at):
        port, slot, item = self.sends[at]
        self.hold(item)
        self.copy(port, slot, item).start()

    def finish(self):
        for item in self.arrives:
            self.hold(item)
        for port, slot, item in self.sends:
            self.copy(port, slot, item).wait_send()


def norm_spread(groups, tall, row_send, row_recv, outward):
    here, n_fsdp = lax.axis_index("fsdp"), groups.shape[0]

    def norm_copy(block, step):
        return pltpu.make_async_remote_copy(
            src_ref=groups.at[here, pl.ds(0, tall)],
            dst_ref=groups.at[block, pl.ds(0, tall)],
            send_sem=row_send.at[step],
            recv_sem=row_recv.at[step],
            device_id={"fsdp": lax.rem(here + step, n_fsdp)},
            device_id_type=MESH,
        )

    if outward:
        return [norm_copy(here, step) for step in range(1, n_fsdp)]
    return [norm_copy(lax.rem(here + n_fsdp - step, n_fsdp), step) for step in range(1, n_fsdp)]


def norm_lines(groups, span, serve_norm):
    out = [None] * serve_norm.shape[0]
    for g in range(groups.shape[0]):
        line = g * span // LANES
        for r in range(-(-(g * span % LANES + span) // LANES)):
            value = groups[g, r : r + 1, :]
            out[line + r] = value if out[line + r] is None else out[line + r] + value
    serve_norm[...] = jnp.concatenate(out, axis=0).astype(serve_norm.dtype)


def first_kernel(n_fsdp, n_cols, *refs):
    bases, lows, highs = refs[0:3], refs[3:6], refs[6:9]
    norm_train, norm_step = refs[9:11]
    gates, ups, downs, group, serve_norm = refs[11:16]
    turned, base_vm, low_vm, high_vm, train_vm, step_vm, sums, parts, groups = refs[16:25]
    send_sem, recv_sem, load_sem, norm_sem, col_send, col_recv, row_send, row_recv = refs[25:]
    here, col = lax.axis_index("fsdp"), lax.axis_index("cols")
    core = lax.rem(col, 2)

    def start_exchange(order, count):
        return Exchange(
            order, bases[:count], lows[:count], highs[:count], base_vm, low_vm, high_vm, (turned, gates, ups)[:count],
            send_sem, recv_sem, load_sem,
        )

    norm_loads = [
        pltpu.make_async_copy(norm_train, train_vm, norm_sem.at[0]),
        pltpu.make_async_copy(norm_step, step_vm, norm_sem.at[1]),
    ]
    barrier = pltpu.get_barrier_semaphore()
    targets, partners = targets_of(here), partners_of(col)
    for peer in targets:
        pl.semaphore_signal(barrier, inc=1, device_id={"fsdp": peer}, device_id_type=MESH)
    for peer in partners:
        pl.semaphore_signal(barrier, inc=1, device_id={"cols": peer}, device_id_type=MESH)

    length = train_vm.shape[0]
    span = n_cols * length
    tall = -(-(span + LANES - 1) // LANES)

    def exchange(step):
        return pltpu.make_async_remote_copy(
            src_ref=sums.at[step, pl.ds(0, tall)],
            dst_ref=parts.at[step, pl.ds(0, tall)],
            send_sem=col_send.at[step],
            recv_sem=col_recv.at[step],
            device_id={"cols": partners[step]},
            device_id_type=MESH,
        )

    def norm_begin():
        for load in norm_loads:
            load.wait()
        flat = LANES * lax.broadcasted_iota(jnp.int32, (8, LANES), 0) + lax.broadcasted_iota(jnp.int32, (8, LANES), 1)
        first = lax.rem(here * span, LANES) + col * length
        tile = jnp.zeros((8, LANES), jnp.float32)
        for j in range(length):
            tile = jnp.where(flat == first + j, train_vm[j] + step_vm[j], tile)
        sums[0] = tile
        exchange(0).start()

    def norm_go_on(step):
        exchange(step - 1).wait()
        sums[step, 0:tall] = sums[step - 1, 0:tall] + parts[step - 1, 0:tall]
        exchange(step).start()

    def turn(x, at, windows):
        for item in x.arrives:
            if item[2] == 0:
                x.hold(item)
        for w in windows:
            downs[:, LANES * w : LANES * (w + 1)] = turned[LANES * w : LANES * (w + 1), :].T

    windows = range(turned.shape[0] // LANES)

    @pl.when(core == 0)
    def _():
        x = start_exchange(WHOLE, 3)
        for load in norm_loads:
            load.start()
        x.merge(0)
        pl.semaphore_wait(barrier, len(targets) + len(partners))
        for at in range(len(x.sends)):
            x.send(at)
            if at == 5:
                norm_begin()
            if at in NORM_AT:
                norm_go_on(NORM_AT.index(at) + 1)
            if at == 30:
                turn(x, at, ())
                exchange(3).wait()
                groups[here, 0:tall] = sums[3, 0:tall] + parts[3, 0:tall]
                for copy in norm_spread(groups, tall, row_send, row_recv, True):
                    copy.start()
            if at > 30:
                turn(x, at, windows[2 * (at - 31) : 2 * (at - 30)])
            if at == 43:
                for copy in norm_spread(groups, tall, row_send, row_recv, False):
                    copy.wait()
                norm_lines(groups, span, serve_norm)
        turn(x, at, windows[2 * (len(x.sends) - 31) :])
        x.finish()

    @pl.when(core == 1)
    def _():
        x = start_exchange(FIRST, 2)
        for load in norm_loads:
            load.start()
        x.merge(0)
        pl.semaphore_wait(barrier, len(targets) + len(partners))
        for at in range(len(x.sends)):
            x.send(at)
            if at == 5:
                norm_begin()
            if at in NORM_AT:
                norm_go_on(NORM_AT.index(at) + 1)
        exchange(3).wait()
        group[...] = jnp.zeros_like(group)
        group[0:tall] = sums[3, 0:tall] + parts[3, 0:tall]
        turn(x, at, windows)
        x.finish()


def second_kernel(n_fsdp, n_cols, length, *refs):
    bases, lows, highs, group = refs[0:1], refs[1:2], refs[2:3], refs[3]
    ups, serve_norm = refs[4:6]
    base_vm, low_vm, high_vm, groups = refs[6:10]
    send_sem, recv_sem, load_sem, row_send, row_recv = refs[10:]
    here, col = lax.axis_index("fsdp"), lax.axis_index("cols")
    barrier = pltpu.get_barrier_semaphore()
    targets = targets_of(here)
    span = n_cols * length
    tall = -(-(span + LANES - 1) // LANES)

    @pl.when(lax.rem(col, 2) == 1)
    def _():
        for peer in targets:
            pl.semaphore_signal(barrier, inc=1, device_id={"fsdp": peer}, device_id_type=MESH)
        x = Exchange(SECOND, bases, lows, highs, base_vm, low_vm, high_vm, (ups,), send_sem, recv_sem, load_sem)
        groups[here] = group[...]
        x.merge(0)
        pl.semaphore_wait(barrier, len(targets))
        place, side = lax.div(here, 2), lax.rem(here, 2)

        def across(block):
            return pltpu.make_async_remote_copy(
                src_ref=groups.at[here, pl.ds(0, tall)],
                dst_ref=groups.at[block, pl.ds(0, tall)],
                send_sem=row_send.at[0],
                recv_sem=row_recv.at[0],
                device_id={"fsdp": targets[2]},
                device_id_type=MESH,
            )

        def along(first, step):
            return pltpu.make_async_remote_copy(
                src_ref=groups.at[pl.ds(2 * place, 2), pl.ds(0, tall)],
                dst_ref=groups.at[pl.ds(2 * first, 2), pl.ds(0, tall)],
                send_sem=row_send.at[step],
                recv_sem=row_recv.at[step],
                device_id={"fsdp": 2 * lax.rem(place + step, DEPTH) + side},
                device_id_type=MESH,
            )

        across(here).start()
        for at in range(len(x.sends)):
            x.send(at)
            if at == len(x.sends) - 3:
                for o in range(1, DEPTH):
                    x.hold(next(i for i in [t[2] for t in x.sends] + list(x.arrives) if i[:2] == (0, o) and i in x.arrives))
                across(2 * place + 1 - side).wait()
                for step in range(1, DEPTH):
                    along(place, step).start()
        x.finish()
        for step in range(1, DEPTH):
            along(lax.rem(place + DEPTH - step, DEPTH), step).wait()
        norm_lines(groups, span, serve_norm)


ANYWHERE = pl.BlockSpec(memory_space=pl.ANY)
INSIDE = pl.BlockSpec(memory_space=pltpu.VMEM)
DMA = pltpu.SemaphoreType.DMA
MIB = 2**20
PARTS = 4


def first(n_fsdp, n_cols, bases, lows, highs, norm_train, norm_step):
    rows, width = bases[0].shape
    rank = lows[0].shape[0]
    bf16, f32 = jnp.bfloat16, jnp.float32
    slots = len(WHOLE) // 3
    return pl.pallas_call(
        functools.partial(first_kernel, n_fsdp, n_cols),
        out_shape=[
            pltpu.VMEM((n_fsdp * rows, width), bf16),
            pltpu.VMEM((n_fsdp * rows, width), bf16),
            pltpu.VMEM((width, n_fsdp * rows), bf16),
            pltpu.VMEM((8, LANES), f32),
            pltpu.VMEM((n_fsdp * n_cols * norm_train.shape[0] // LANES, LANES), bf16),
        ],
        in_specs=[ANYWHERE] * 11,
        out_specs=[INSIDE] * 5,
        scratch_shapes=[
            pltpu.VMEM((n_fsdp * rows, width), bf16),
            pltpu.VMEM((3, rows, width), bf16),
            pltpu.VMEM((3, rank, rows), bf16),
            pltpu.VMEM((3, rank, width), bf16),
            pltpu.SMEM(norm_train.shape, f32),
            pltpu.SMEM(norm_step.shape, f32),
            pltpu.VMEM((4, 8, LANES), f32),
            pltpu.VMEM((4, 8, LANES), f32),
            pltpu.VMEM((n_fsdp, 8, LANES), f32),
            DMA((3, slots)),
            DMA((3, slots)),
            DMA((3, 3)),
            DMA((2,)),
            DMA((4,)),
            DMA((4,)),
            DMA((n_fsdp,)),
            DMA((n_fsdp,)),
        ],
        compiler_params=pltpu.CompilerParams(collective_id=0, has_side_effects=True, vmem_limit_bytes=42 * MIB),
    )(*bases, *lows, *highs, norm_train, norm_step)


def second(n_fsdp, n_cols, length, base, low, high, group):
    rows, width = base.shape
    rank = low.shape[0]
    bf16, f32 = jnp.bfloat16, jnp.float32
    slots = len(SECOND) // 3
    return pl.pallas_call(
        functools.partial(second_kernel, n_fsdp, n_cols, length),
        out_shape=[
            pltpu.VMEM((n_fsdp * rows, width), bf16),
            pltpu.VMEM((n_fsdp * n_cols * length // LANES, LANES), bf16),
        ],
        in_specs=[ANYWHERE] * 3 + [INSIDE],
        out_specs=[INSIDE] * 2,
        scratch_shapes=[
            pltpu.VMEM((1, rows, width), bf16),
            pltpu.VMEM((1, rank, rows), bf16),
            pltpu.VMEM((1, rank, width), bf16),
            pltpu.VMEM((n_fsdp, 8, LANES), f32),
            DMA((3, slots)),
            DMA((3, slots)),
            DMA((1, 3)),
            DMA((n_fsdp,)),
            DMA((n_fsdp,)),
        ],
        compiler_params=pltpu.CompilerParams(collective_id=1, has_side_effects=True, vmem_limit_bytes=50 * MIB),
    )(base, low, high, group)


def run_copies(refs, sem):
    copies = []
    for a, (src, dst, parts) in enumerate(refs):
        rows = src.shape[0] // parts
        for p in range(parts):
            part = pl.ds(p * rows, rows)
            copies.append(pltpu.make_async_copy(src.at[part], dst.at[part], sem.at[a, p]))
    for c in copies:
        c.start()
    for c in copies:
        c.wait()


def write_first_kernel(gates, ups, downs, norm, group, gates_out, ups_out, downs_out, norm_out, group_out, sem):
    core = lax.rem(lax.axis_index("cols"), 2)
    group_out[...] = group[...]
    both = [(gates, gates_out, PARTS), (downs, downs_out, PARTS)]

    @pl.when(core == 0)
    def _():
        run_copies(both + [(ups, ups_out, PARTS), (norm, norm_out, 1)], sem)

    @pl.when(core == 1)
    def _():
        run_copies(both, sem)


def write_first(gates, ups, downs, norm, group):
    arrays = (gates, ups, downs, norm)
    return pl.pallas_call(
        write_first_kernel,
        out_shape=[jax.ShapeDtypeStruct(a.shape, a.dtype) for a in arrays] + [pltpu.VMEM(group.shape, group.dtype)],
        in_specs=[INSIDE] * 5,
        out_specs=[ANYWHERE] * 4 + [INSIDE],
        scratch_shapes=[DMA((4, PARTS))],
        compiler_params=pltpu.CompilerParams(vmem_limit_bytes=8 * MIB),
    )(*arrays, group)


def write_second_kernel(ups, norm, ups_in, norm_in, ups_out, norm_out, sem):
    del ups_in, norm_in

    @pl.when(lax.rem(lax.axis_index("cols"), 2) == 1)
    def _():
        run_copies([(ups, ups_out, PARTS), (norm, norm_out, 1)], sem)


def write_second(ups, norm, ups_out, norm_out):
    return pl.pallas_call(
        write_second_kernel,
        out_shape=[jax.ShapeDtypeStruct(a.shape, a.dtype) for a in (ups_out, norm_out)],
        in_specs=[INSIDE] * 2 + [ANYWHERE] * 2,
        out_specs=[ANYWHERE] * 2,
        input_output_aliases={2: 0, 3: 1},
        scratch_shapes=[DMA((2, PARTS))],
        compiler_params=pltpu.CompilerParams(vmem_limit_bytes=8 * MIB),
    )(ups, norm, ups_out, norm_out)


def per_device(
    n_fsdp,
    n_cols,
    train_gate,
    low_gate,
    high_gate,
    train_up,
    low_up,
    high_up,
    train_down,
    low_down,
    high_down,
    norm_train,
    norm_step,
):
    gates, ups, downs, group, norm = first(
        n_fsdp,
        n_cols,
        (train_down.T, train_gate, train_up),
        (high_down, low_gate.T, low_up.T),
        (low_down.T, high_gate, high_up),
        norm_train,
        norm_step,
    )
    gates, ups, downs, norm, group = write_first(gates, ups, downs, norm, group)
    late_ups, late_norm = second(n_fsdp, n_cols, norm_train.shape[0], train_up, low_up.T, high_up, group)
    ups, norm = write_second(late_ups, late_norm, ups, norm)
    return gates, ups, downs, norm.reshape(-1)


def solution(mesh):
    return jax.shard_map(
        functools.partial(per_device, mesh.shape["fsdp"], mesh.shape["cols"]),
        mesh=mesh,
        in_specs=(
            P("fsdp", "cols"),
            P("fsdp", None),
            P(None, "cols"),
            P("fsdp", "cols"),
            P("fsdp", None),
            P(None, "cols"),
            P("cols", "fsdp"),
            P("cols", None),
            P(None, "fsdp"),
            P(("fsdp", "cols")),
            P(("fsdp", "cols")),
        ),
        out_specs=(P(None, "cols"), P(None, "cols"), P("cols", None), P()),
        check_vma=False,
    )
```

time: 148 us -> 144 us (0.973)
  Pallas kernels: 147 us -> 143 us
    pallas_call x2 -> x4, Pallas kernels: 147 us -> 143 us  [the longest x1 96.8 us: first(): pl.pallas_call(functools.partial(first_kernel, n_fsdp, n_cols), out_shape...]
where the time goes in v3:
time: 144 us
  Pallas kernels  143 us (99%)
    pallas_call x1, Pallas kernels, first(): pl.pallas_call(functools.partial(first_kernel, n_fsdp, n_cols), out_shape...  96.8 us
    pallas_call x1, Pallas kernels, second(): pl.pallas_call(functools.partial(second_kernel, n_fsdp, n_cols, length),...  38.5 us
    pallas_call x1, Pallas kernels, write_first(): pl.pallas_call(write_first_kernel, out_shape=[jax.ShapeDtypeStruct(a.shap...  4.85 us

profile of v3, /device:TPU:1, one launch (start us, length us, event | category | flops | bytes accessed | tf_op | source)
XLA Modules:
  0.0 144.3 jit_solution(14930511885658048713)
XLA Ops:
  0.6 96.8 %shard_map.138 = (bf16[3584,896]{1,0:T(8,128)(2,1)S(1)}, bf16[3584,896]{1,0:T(8,128)(2,1)S(1)}, bf16[896,3584]{1,0:T(8,128)(2,1)S(1)}, f32[8,128]{1,0:T(8,128)S(1)}, bf16[28,128]{1,0:T(8,128)(2,1)S(1)}) custom-call(bf16[224,896]{1,0:T(8,128)(2,1)} %bitcast.5, bf16[224,896]{1,0:T(8,128)(2,1)} %refs_1_.1, bf16[224,896]{1,0:T(8,128)(2,1)} %refs_0_.1, ...), custom_call_target="tpu_custom_call" | custom-call | tf_op jit(solution)/shard_map/pallas_call | solution.py:362
  97.5 4.8 %shard_map.139 = (bf16[3584,896]{1,0:T(8,128)(2,1)}, bf16[3584,896]{1,0:T(8,128)(2,1)}, bf16[896,3584]{1,0:T(8,128)(2,1)}, bf16[28,128]{1,0:T(8,128)(2,1)}, f32[8,128]{1,0:T(8,128)S(1)}) custom-call(bf16[3584,896]{1,0:T(8,128)(2,1)S(1)} %get-tuple-element.18.gates, bf16[3584,896]{1,0:T(8,128)(2,1)S(1)} %get-tuple-element.19.ups, ...), custom_call_target="tpu_custom_call" | custom-call | tf_op jit(solution)/shard_map/pallas_call | solution.py:453
  102.3 0.0 copy-start
  102.3 0.6 copy-done
  102.9 38.5 %shard_map.140 = (bf16[3584,896]{1,0:T(8,128)(2,1)S(1)}, bf16[28,128]{1,0:T(8,128)(2,1)S(1)}) custom-call(bf16[224,896]{1,0:T(8,128)(2,1)} %refs_0_.1, bf16[16,224]{1,0:T(8,128)(2,1)} %bitcast.7, bf16[16,896]{1,0:T(8,128)(2,1)} %refs_2_.3, f32[8,128]{1,0:T(8,128)} %copy-done), custom_call_target="tpu_custom_call" | custom-call | tf_op jit(solution)/shard_map/pallas_call | solution.py:401
  141.4 2.8 %shard_map.141 = (bf16[3584,896]{1,0:T(8,128)(2,1)}, bf16[28,128]{1,0:T(8,128)(2,1)}) custom-call(bf16[3584,896]{1,0:T(8,128)(2,1)S(1)} %get-tuple-element.25.ups, bf16[28,128]{1,0:T(8,128)(2,1)S(1)} %get-tuple-element.26.norm, bf16[3584,896]{1,0:T(8,128)(2,1)} %get-tuple-element.27.ups_in, ...), custom_call_target="tpu_custom_call", output_to_operand_aliasing={{0}: (2, {}), {1}: (3, {})} | custom-call | tf_op jit(solution)/shard_map/pallas_call | solution.py:472
Async XLA Ops:
  102.3 0.6 copy-start

commit v4 on v2

--- a/solution.py
+++ b/solution.py
@@ -24,7 +24,9 @@
     (2, 1, 6, 2), (0, 1, 5, 1), (1, 0, 2, 1),
 )
 SLOTS = len(ORDER) // 3
-NORM_AT = (6, 8, 10, 12)
+LATE = 6
+NORM_AT = (8, 10, 12)
+NORM_SPREAD_AT, NORM_LAST_AT = 30, len(ORDER) - LATE - 1
 WRITES = 4
 
 
@@ -60,17 +62,37 @@
     )
 
 
+def targets_of(here):
+    place, side = lax.div(here, 2), lax.rem(here, 2)
+    return (
+        2 * lax.rem(place + 1, DEPTH) + side,
+        2 * lax.rem(place + DEPTH - 1, DEPTH) + side,
+        2 * place + 1 - side,
+    )
+
+
+def rows_of(item, rows):
+    here = lax.axis_index("fsdp")
+    place, side = lax.div(here, 2), lax.rem(here, 2)
+    column, offset = item[:2]
+    block = 2 * lax.rem(place + offset, DEPTH) + (side if column == 0 else 1 - side)
+    return pl.ds(pl.multiple_of(block * rows, 32), rows)
+
+
+def is_core(core):
+    return lax.rem(lax.axis_index("cols"), 2) == core
+
+
 def gather_kernel(n_fsdp, n_cols, *refs):
     bases, lows, highs = refs[0:3], refs[3:6], refs[6:9]
     norm_train, norm_step = refs[9:11]
     gates, ups, downs, serve_norm = refs[11:15]
     turned, base_vm, low_vm, high_down, high_gate, high_up, train_vm, step_vm, sums, parts, groups = refs[15:26]
-    send_sem, recv_sem, local_sem, col_send, col_recv, row_send, row_recv = refs[26:]
+    send_sem, recv_sem, local_sem, col_send, col_recv, row_send, row_recv, lead_sem = refs[26:]
     high_vm = (high_down, high_gate, high_up)
     wholes = (turned, gates, ups)
     rows = base_vm.shape[1]
     here, col = lax.axis_index("fsdp"), lax.axis_index("cols")
-    place, side = lax.div(here, 2), lax.rem(here, 2)
 
     loads = [
         pltpu.make_async_copy(src, dst, local_sem.at[s])
@@ -83,19 +105,15 @@
         load.start()
 
     barrier = pltpu.get_barrier_semaphore()
-    targets = (2 * lax.rem(place + 1, DEPTH) + side, 2 * lax.rem(place + DEPTH - 1, DEPTH) + side, 2 * place + 1 - side)
+    targets = targets_of(here)
     for peer in targets:
         pl.semaphore_signal(barrier, inc=1, device_id={"fsdp": peer}, device_id_type=MESH)
     partners = partners_of(col)
     for peer in partners:
         pl.semaphore_signal(barrier, inc=1, device_id={"cols": peer}, device_id_type=MESH)
 
-    def block_of(column, offset):
-        return 2 * lax.rem(place + offset, DEPTH) + (side if column == 0 else 1 - side)
-
     def where(column, offset, piece):
-        start = pl.multiple_of(block_of(column, offset) * rows, 32)
-        return wholes[piece].at[pl.ds(start, rows)]
+        return wholes[piece].at[rows_of((column, offset), rows)]
 
     def merge(c):
         for load in loads[3 * c : 3 * c + 3]:
@@ -192,31 +210,134 @@
 
     hold((0, 0, 0))
     pl.semaphore_wait(barrier, len(targets) + len(partners))
+
+    @pl.when(is_core(0))
+    def _():
+        norm_step_at(0)
+        pl.semaphore_wait(lead_sem, 1)
+
     downs_in = [item for item in arrives if item[2] == 0]
     windows = list(range(n_fsdp * rows // LANES))
-    ready = None
-    for at, (port, slot, item) in enumerate(sends):
+    early, late = sends[:-LATE], sends[-LATE:]
+    for at, (port, slot, item) in enumerate(early):
         hold(item)
         copy(port, slot, item).start()
+        if at == 5:
+
+            @pl.when(is_core(1))
+            def _():
+                norm_step_at(0)
+                copy(*sends[0]).wait_send()
+                pl.semaphore_signal(lead_sem, inc=1, device_id={"cols": partners[0]}, device_id_type=MESH)
+
         if at in NORM_AT:
-            norm_step_at(NORM_AT.index(at))
-        if at == 30:
+            norm_step_at(NORM_AT.index(at) + 1)
+        if at == NORM_SPREAD_AT:
             for i in downs_in:
                 hold(i)
-            ready = at
             norm_spread()
-        if at == 43:
+        if at == NORM_LAST_AT:
             norm_last()
-        if ready is not None:
-            for w in windows[:2]:
+        if at >= NORM_SPREAD_AT:
+            for w in windows[:3]:
                 turn(w)
-            del windows[:2]
+            del windows[:3]
     for w in windows:
         turn(w)
-    for item in arrives:
-        hold(item)
-    for port, slot, item in sends:
-        copy(port, slot, item).wait_send()
+    before = set(held)
+
+    @pl.when(is_core(0))
+    def _():
+        for port, slot, item in late:
+            hold(item)
+            copy(port, slot, item).start()
+        for item in arrives:
+            hold(item)
+        for each in sends:
+            copy(*each).wait_send()
+
+    held.clear()
+    held.update(before)
+
+    @pl.when(is_core(1))
+    def _():
+        for item in arrives:
+            if item not in [received(port, *item) for port, _, item in late]:
+                hold(item)
+        for each in early[1:]:
+            copy(*each).wait_send()
+
+
+def late_kernel(gates, ups, token, arrived, send_sem, recv_sem):
+    del token
+    targets = targets_of(lax.axis_index("fsdp"))
+    barrier = pltpu.get_barrier_semaphore()
+
+    @pl.when(is_core(1))
+    def _():
+        for peer in targets:
+            pl.semaphore_signal(barrier, inc=1, device_id={"fsdp": peer}, device_id_type=MESH)
+        pl.semaphore_wait(barrier, len(targets))
+        copies = []
+        for n, (port, *item) in enumerate(ORDER[-LATE:]):
+            whole = gates if item[2] == 1 else ups
+            copies.append(
+                pltpu.make_async_remote_copy(
+                    src_ref=whole.at[rows_of(item, arrived.shape[1])],
+                    dst_ref=arrived.at[n],
+                    send_sem=send_sem.at[n],
+                    recv_sem=recv_sem.at[n],
+                    device_id={"fsdp": targets[port]},
+                    device_id_type=MESH,
+                )
+            )
+        for c in copies:
+            c.start()
+        for c in copies:
+            c.wait()
+
+
+def send_late(gates, ups, token):
+    inside = pl.BlockSpec(memory_space=pltpu.VMEM)
+    return pl.pallas_call(
+        late_kernel,
+        out_shape=pltpu.VMEM((LATE, gates.shape[0] // (2 * DEPTH), gates.shape[1]), gates.dtype),
+        in_specs=[inside] * 3,
+        out_specs=inside,
+        scratch_shapes=[pltpu.SemaphoreType.DMA((LATE,)), pltpu.SemaphoreType.DMA((LATE,))],
+        compiler_params=pltpu.CompilerParams(collective_id=1, has_side_effects=True, vmem_limit_bytes=8 * 2**20),
+    )(*(pltpu.with_memory_space_constraint(a, pltpu.VMEM) for a in (gates, ups, token)))
+
+
+def write_late_kernel(arrived, gates_in, ups_in, gates_out, ups_out, sem):
+    del gates_in, ups_in
+
+    @pl.when(is_core(1))
+    def _():
+        copies = []
+        for n, (port, *item) in enumerate(ORDER[-LATE:]):
+            item = received(port, *item)
+            whole = gates_out if item[2] == 1 else ups_out
+            copies.append(
+                pltpu.make_async_copy(arrived.at[n], whole.at[rows_of(item, arrived.shape[1])], sem.at[n])
+            )
+        for c in copies:
+            c.start()
+        for c in copies:
+            c.wait()
+
+
+def write_late(arrived, gates, ups):
+    anywhere = pl.BlockSpec(memory_space=pl.ANY)
+    return pl.pallas_call(
+        write_late_kernel,
+        out_shape=[jax.ShapeDtypeStruct(a.shape, a.dtype) for a in (gates, ups)],
+        in_specs=[pl.BlockSpec(memory_space=pltpu.VMEM), anywhere, anywhere],
+        out_specs=[anywhere] * 2,
+        input_output_aliases={1: 0, 2: 1},
+        scratch_shapes=[pltpu.SemaphoreType.DMA((LATE,))],
+        compiler_params=pltpu.CompilerParams(vmem_limit_bytes=8 * 2**20),
+    )(arrived, gates, ups)
 
 
 def gather(n_fsdp, n_cols, bases, lows, highs, norm_train, norm_step):
@@ -256,13 +377,15 @@
             dma((4,)),
             dma((n_fsdp,)),
             dma((n_fsdp,)),
+            pltpu.SemaphoreType.REGULAR,
         ],
         compiler_params=pltpu.CompilerParams(collective_id=0, has_side_effects=True, vmem_limit_bytes=42 * 2**20),
     )(*bases, *lows, *highs, norm_train, norm_step)
 
 
 def write_kernel(*refs):
-    ins, outs, sem = refs[:4], refs[4:8], refs[8]
+    ins, outs, token, sem = refs[:4], refs[4:8], refs[8], refs[9]
+    token[...] = jnp.zeros_like(token)
     parts = sem.shape[1]
     copies = [pltpu.make_async_copy(ins[3], outs[3], sem.at[3, 0])]
     for p in range(parts):
@@ -279,9 +402,9 @@
 def write(arrays):
     return pl.pallas_call(
         write_kernel,
-        out_shape=[jax.ShapeDtypeStruct(a.shape, a.dtype) for a in arrays],
+        out_shape=[jax.ShapeDtypeStruct(a.shape, a.dtype) for a in arrays] + [pltpu.VMEM((8, LANES), jnp.float32)],
         in_specs=[pl.BlockSpec(memory_space=pltpu.VMEM)] * 4,
-        out_specs=[pl.BlockSpec(memory_space=pl.ANY)] * 4,
+        out_specs=[pl.BlockSpec(memory_space=pl.ANY)] * 4 + [pl.BlockSpec(memory_space=pltpu.VMEM)],
         scratch_shapes=[pltpu.SemaphoreType.DMA((4, WRITES))],
         compiler_params=pltpu.CompilerParams(vmem_limit_bytes=8 * 2**20),
     )(*arrays)
@@ -311,7 +434,8 @@
         norm_train,
         norm_step,
     )
-    gates, ups, downs, norm = write((gates, ups, downs, norm))
+    gates_out, ups_out, downs, norm, token = write((gates, ups, downs, norm))
+    gates, ups = write_late(send_late(gates, ups, token), gates_out, ups_out)
     return gates, ups, downs, norm.reshape(-1)
 
 

time: 148 us -> 142 us (0.959)
  Pallas kernels: 147 us -> 141 us
    pallas_call x1, Pallas kernels: 140 us -> 119 us  [gather(): pl.pallas_call(functools.partial(gather_kernel, n_fsdp, n_cols), out_shap...]
    pallas_call x0 -> x2, Pallas kernels: none -> 15.9 us  [the longest x1 14.5 us: send_late(): pl.pallas_call(late_kernel, out_shape=pltpu.VMEM((LATE, gates.shape[0] //...]
where the time goes in v4:
time: 142 us
  Pallas kernels  141 us (99%)
    pallas_call x1, Pallas kernels, gather(): pl.pallas_call(functools.partial(gather_kernel, n_fsdp, n_cols), out_shap...  119 us
    pallas_call x1, Pallas kernels, send_late(): pl.pallas_call(late_kernel, out_shape=pltpu.VMEM((LATE, gates.shape[0] //...  14.5 us
    pallas_call x1, Pallas kernels, write(): pl.pallas_call(write_kernel, out_shape=[jax.ShapeDtypeStruct(a.shape, a.d...  6.75 us

profile of v4, /device:TPU:1, one launch (start us, length us, event | category | flops | bytes accessed | tf_op | source)
XLA Modules:
  0.0 142.1 jit_solution(9196947656280605676)
XLA Ops:
  0.6 118.8 %shard_map.138 = (bf16[3584,896]{1,0:T(8,128)(2,1)S(1)}, bf16[3584,896]{1,0:T(8,128)(2,1)S(1)}, bf16[896,3584]{1,0:T(8,128)(2,1)S(1)}, bf16[28,128]{1,0:T(8,128)(2,1)S(1)}) custom-call(bf16[224,896]{1,0:T(8,128)(2,1)} %bitcast.5, bf16[224,896]{1,0:T(8,128)(2,1)} %refs_1_.1, bf16[224,896]{1,0:T(8,128)(2,1)} %refs_2_.1, bf16[16,224]{1,0:T(8,128)(2,1)} %refs_3_.1, ...), custom_call_target="tpu_custom_call" | custom-call | tf_op jit(solution)/shard_map/pallas_call | solution.py:351
  119.4 6.7 %shard_map.139 = (bf16[3584,896]{1,0:T(8,128)(2,1)}, bf16[3584,896]{1,0:T(8,128)(2,1)}, bf16[896,3584]{1,0:T(8,128)(2,1)}, bf16[28,128]{1,0:T(8,128)(2,1)}, f32[8,128]{1,0:T(8,128)S(1)}) custom-call(bf16[3584,896]{1,0:T(8,128)(2,1)S(1)} %get-tuple-element.15.refs_0_.gates, bf16[3584,896]{1,0:T(8,128)(2,1)S(1)} %get-tuple-element.16.refs_1_.ups, ...), custom_call_target="tpu_custom_call" | custom-call | tf_op jit(solution)/shard_map/pallas_call | solution.py:403
  126.2 14.5 %shard_map.140.arrived = bf16[6,224,896]{2,1,0:T(8,128)(2,1)S(1)} custom-call(bf16[3584,896]{1,0:T(8,128)(2,1)S(1)} %get-tuple-element.15.refs_0_.gates, bf16[3584,896]{1,0:T(8,128)(2,1)S(1)} %get-tuple-element.16.refs_1_.ups, f32[8,128]{1,0:T(8,128)S(1)} %get-tuple-element.19.token), custom_call_target="tpu_custom_call" | custom-call | tf_op jit(solution)/shard_map/pallas_call | solution.py:302
  140.6 1.5 %shard_map.141 = (bf16[3584,896]{1,0:T(8,128)(2,1)}, bf16[3584,896]{1,0:T(8,128)(2,1)}) custom-call(bf16[6,224,896]{2,1,0:T(8,128)(2,1)S(1)} %shard_map.140.arrived, bf16[3584,896]{1,0:T(8,128)(2,1)} %get-tuple-element.20.gates_in, bf16[3584,896]{1,0:T(8,128)(2,1)} %get-tuple-element.21.ups_in), custom_call_target="tpu_custom_call", output_to_operand_aliasing={{0}: (1, {}), {1}: (2, {})} | custom-call | tf_op jit(solution)/shard_map/pallas_call | solution.py:332

commit v5 on v4

--- a/solution.py
+++ b/solution.py
@@ -26,7 +26,7 @@
 SLOTS = len(ORDER) // 3
 LATE = 6
 NORM_AT = (8, 10, 12)
-NORM_SPREAD_AT, NORM_LAST_AT = 30, len(ORDER) - LATE - 1
+NORM_ACROSS_AT, NORM_SPREAD_AT, NORM_LAST_AT = 17, 30, len(ORDER) - LATE - 1
 WRITES = 4
 
 
@@ -101,9 +101,6 @@
             + [(norm_train, train_vm), (norm_step, step_vm)]
         )
     ]
-    for load in loads:
-        load.start()
-
     barrier = pltpu.get_barrier_semaphore()
     targets = targets_of(here)
     for peer in targets:
@@ -111,6 +108,8 @@
     partners = partners_of(col)
     for peer in partners:
         pl.semaphore_signal(barrier, inc=1, device_id={"cols": peer}, device_id_type=MESH)
+    for load in loads:
+        load.start()
 
     def where(column, offset, piece):
         return wholes[piece].at[rows_of((column, offset), rows)]
@@ -180,25 +179,41 @@
             sums[step, 0:tall] = sums[step - 1, 0:tall] + parts[step - 1, 0:tall]
         exchange(step).start()
 
-    def norm_copy(block, step):
+    place, side = lax.div(here, 2), lax.rem(here, 2)
+
+    def across(block):
         return pltpu.make_async_remote_copy(
             src_ref=groups.at[here, pl.ds(0, tall)],
             dst_ref=groups.at[block, pl.ds(0, tall)],
+            send_sem=row_send.at[0],
+            recv_sem=row_recv.at[0],
+            device_id={"fsdp": targets[2]},
+            device_id_type=MESH,
+        )
+
+    def along(start, step):
+        return pltpu.make_async_remote_copy(
+            src_ref=groups.at[pl.ds(2 * place, 2), pl.ds(0, tall)],
+            dst_ref=groups.at[pl.ds(2 * start, 2), pl.ds(0, tall)],
             send_sem=row_send.at[step],
             recv_sem=row_recv.at[step],
-            device_id={"fsdp": lax.rem(here + step, n_fsdp)},
+            device_id={"fsdp": 2 * lax.rem(place + step, DEPTH) + side},
             device_id_type=MESH,
         )
 
-    def norm_spread():
+    def norm_across():
         exchange(3).wait()
         groups[here, 0:tall] = sums[3, 0:tall] + parts[3, 0:tall]
-        for step in range(1, n_fsdp):
-            norm_copy(here, step).start()
+        across(here).start()
+
+    def norm_spread():
+        across(2 * place + 1 - side).wait()
+        for step in range(1, DEPTH):
+            along(place, step).start()
 
     def norm_last():
-        for step in range(1, n_fsdp):
-            norm_copy(lax.rem(here + n_fsdp - step, n_fsdp), step).wait()
+        for step in range(1, DEPTH):
+            along(lax.rem(place + DEPTH - step, DEPTH), step).wait()
         lines = serve_norm.shape[0]
         out = [None] * lines
         for g in range(n_fsdp):
@@ -232,6 +247,8 @@
 
         if at in NORM_AT:
             norm_step_at(NORM_AT.index(at) + 1)
+        if at == NORM_ACROSS_AT:
+            norm_across()
         if at == NORM_SPREAD_AT:
             for i in downs_in:
                 hold(i)
@@ -375,8 +392,8 @@
             dma((3 * PIECES + 2,)),
             dma((4,)),
             dma((4,)),
-            dma((n_fsdp,)),
-            dma((n_fsdp,)),
+            dma((DEPTH,)),
+            dma((DEPTH,)),
             pltpu.SemaphoreType.REGULAR,
         ],
         compiler_params=pltpu.CompilerParams(collective_id=0, has_side_effects=True, vmem_limit_bytes=42 * 2**20),

time: 142 us -> 142 us (level)
  no operation moved by 1% of the time
where the time goes in v5:
time: 142 us
  Pallas kernels  141 us (99%)
    pallas_call x1, Pallas kernels, gather(): pl.pallas_call(functools.partial(gather_kernel, n_fsdp, n_cols), out_shap...  119 us
    pallas_call x1, Pallas kernels, send_late(): pl.pallas_call(late_kernel, out_shape=pltpu.VMEM((LATE, gates.shape[0] //...  14.6 us
    pallas_call x1, Pallas kernels, write(): pl.pallas_call(write_kernel, out_shape=[jax.ShapeDtypeStruct(a.shape, a.d...  6.75 us

profile of v5, /device:TPU:1, one launch (start us, length us, event | category | flops | bytes accessed | tf_op | source)
XLA Modules:
  0.0 142.1 jit_solution(13695361327855388603)
XLA Ops:
  0.6 118.6 %shard_map.138 = (bf16[3584,896]{1,0:T(8,128)(2,1)S(1)}, bf16[3584,896]{1,0:T(8,128)(2,1)S(1)}, bf16[896,3584]{1,0:T(8,128)(2,1)S(1)}, bf16[28,128]{1,0:T(8,128)(2,1)S(1)}) custom-call(bf16[224,896]{1,0:T(8,128)(2,1)} %bitcast.5, bf16[224,896]{1,0:T(8,128)(2,1)} %refs_1_.1, bf16[224,896]{1,0:T(8,128)(2,1)} %refs_2_.1, bf16[16,224]{1,0:T(8,128)(2,1)} %refs_3_.1, ...), custom_call_target="tpu_custom_call" | custom-call | tf_op jit(solution)/shard_map/pallas_call | solution.py:368
  119.3 6.7 %shard_map.139 = (bf16[3584,896]{1,0:T(8,128)(2,1)}, bf16[3584,896]{1,0:T(8,128)(2,1)}, bf16[896,3584]{1,0:T(8,128)(2,1)}, bf16[28,128]{1,0:T(8,128)(2,1)}, f32[8,128]{1,0:T(8,128)S(1)}) custom-call(bf16[3584,896]{1,0:T(8,128)(2,1)S(1)} %get-tuple-element.15.refs_0_.gates, bf16[3584,896]{1,0:T(8,128)(2,1)S(1)} %get-tuple-element.16.refs_1_.ups, ...), custom_call_target="tpu_custom_call" | custom-call | tf_op jit(solution)/shard_map/pallas_call | solution.py:420
  126.0 14.6 %shard_map.140.arrived = bf16[6,224,896]{2,1,0:T(8,128)(2,1)S(1)} custom-call(bf16[3584,896]{1,0:T(8,128)(2,1)S(1)} %get-tuple-element.15.refs_0_.gates, bf16[3584,896]{1,0:T(8,128)(2,1)S(1)} %get-tuple-element.16.refs_1_.ups, f32[8,128]{1,0:T(8,128)S(1)} %get-tuple-element.19.token), custom_call_target="tpu_custom_call" | custom-call | tf_op jit(solution)/shard_map/pallas_call | solution.py:319
  140.6 1.5 %shard_map.141 = (bf16[3584,896]{1,0:T(8,128)(2,1)}, bf16[3584,896]{1,0:T(8,128)(2,1)}) custom-call(bf16[6,224,896]{2,1,0:T(8,128)(2,1)S(1)} %shard_map.140.arrived, bf16[3584,896]{1,0:T(8,128)(2,1)} %get-tuple-element.20.gates_in, bf16[3584,896]{1,0:T(8,128)(2,1)} %get-tuple-element.21.ups_in), custom_call_target="tpu_custom_call", output_to_operand_aliasing={{0}: (1, {}), {1}: (2, {})} | custom-call | tf_op jit(solution)/shard_map/pallas_call | solution.py:349

commit v6 on v5

--- a/solution.py
+++ b/solution.py
@@ -108,7 +108,7 @@
     partners = partners_of(col)
     for peer in partners:
         pl.semaphore_signal(barrier, inc=1, device_id={"cols": peer}, device_id_type=MESH)
-    for load in loads:
+    for load in loads[:3]:
         load.start()
 
     def where(column, offset, piece):
@@ -117,6 +117,9 @@
     def merge(c):
         for load in loads[3 * c : 3 * c + 3]:
             load.wait()
+        if c == 0:
+            for load in loads[3:]:
+                load.start()
         product = lax.dot_general(
             low_vm[c], high_vm[c][...], (((0,), (0,)), ((), ())), preferred_element_type=jnp.float32
         )

time: 142 us -> 142 us (level)
  no operation moved by 1% of the time
where the time goes in v6:
time: 142 us
  Pallas kernels  141 us (99%)
    pallas_call x1, Pallas kernels, gather(): pl.pallas_call(functools.partial(gather_kernel, n_fsdp, n_cols), out_shap...  119 us
    pallas_call x1, Pallas kernels, send_late(): pl.pallas_call(late_kernel, out_shape=pltpu.VMEM((LATE, gates.shape[0] //...  14.6 us
    pallas_call x1, Pallas kernels, write(): pl.pallas_call(write_kernel, out_shape=[jax.ShapeDtypeStruct(a.shape, a.d...  6.75 us

profile of v6, /device:TPU:1, one launch (start us, length us, event | category | flops | bytes accessed | tf_op | source)
XLA Modules:
  0.0 142.1 jit_solution(14223432019006844211)
XLA Ops:
  0.6 118.6 %shard_map.138 = (bf16[3584,896]{1,0:T(8,128)(2,1)S(1)}, bf16[3584,896]{1,0:T(8,128)(2,1)S(1)}, bf16[896,3584]{1,0:T(8,128)(2,1)S(1)}, bf16[28,128]{1,0:T(8,128)(2,1)S(1)}) custom-call(bf16[224,896]{1,0:T(8,128)(2,1)} %bitcast.5, bf16[224,896]{1,0:T(8,128)(2,1)} %refs_1_.1, bf16[224,896]{1,0:T(8,128)(2,1)} %refs_2_.1, bf16[16,224]{1,0:T(8,128)(2,1)} %refs_3_.1, ...), custom_call_target="tpu_custom_call" | custom-call | tf_op jit(solution)/shard_map/pallas_call | solution.py:371
  119.3 6.7 %shard_map.139 = (bf16[3584,896]{1,0:T(8,128)(2,1)}, bf16[3584,896]{1,0:T(8,128)(2,1)}, bf16[896,3584]{1,0:T(8,128)(2,1)}, bf16[28,128]{1,0:T(8,128)(2,1)}, f32[8,128]{1,0:T(8,128)S(1)}) custom-call(bf16[3584,896]{1,0:T(8,128)(2,1)S(1)} %get-tuple-element.15.refs_0_.gates, bf16[3584,896]{1,0:T(8,128)(2,1)S(1)} %get-tuple-element.16.refs_1_.ups, ...), custom_call_target="tpu_custom_call" | custom-call | tf_op jit(solution)/shard_map/pallas_call | solution.py:423
  126.0 14.6 %shard_map.140.arrived = bf16[6,224,896]{2,1,0:T(8,128)(2,1)S(1)} custom-call(bf16[3584,896]{1,0:T(8,128)(2,1)S(1)} %get-tuple-element.15.refs_0_.gates, bf16[3584,896]{1,0:T(8,128)(2,1)S(1)} %get-tuple-element.16.refs_1_.ups, f32[8,128]{1,0:T(8,128)S(1)} %get-tuple-element.19.token), custom_call_target="tpu_custom_call" | custom-call | tf_op jit(solution)/shard_map/pallas_call | solution.py:322
  140.6 1.5 %shard_map.141 = (bf16[3584,896]{1,0:T(8,128)(2,1)}, bf16[3584,896]{1,0:T(8,128)(2,1)}) custom-call(bf16[6,224,896]{2,1,0:T(8,128)(2,1)S(1)} %shard_map.140.arrived, bf16[3584,896]{1,0:T(8,128)(2,1)} %get-tuple-element.20.gates_in, bf16[3584,896]{1,0:T(8,128)(2,1)} %get-tuple-element.21.ups_in), custom_call_target="tpu_custom_call", output_to_operand_aliasing={{0}: (1, {}), {1}: (2, {})} | custom-call | tf_op jit(solution)/shard_map/pallas_call | solution.py:352
